TPU v7x, 128 devices: a whole 4x4x4 slice. The times are simulated.
128 devices in a mesh: dp: 64 (over y, x, z_lo, core), mp: 2 (over z_hi).
Axes of the slice: x: 4, y: 4, z: 4 (z_hi: 2, z_lo: 2; z = z_hi * 2 + z_lo), core: 2. Of those that a mesh axis runs over, the one named last changes fastest.
Arguments:
- clean_latent: float32 [64, 4096], P('dp'), may hold values from -6 to 6
- noise_draw: float32 [64, 4096], P('dp'), may hold values from -6 to 6
- timestep: int32 [64], P('dp'), may hold values from 1 to 8
- bucket: int32 [64], P('dp'), may hold values from 0 to 7
- bucket_weights: float32 [8], replicated, may hold values from 0.25 to 4
- teacher_embed: float32 [16, 2048], replicated, may hold values from -1.5 to 1.5
- teacher_final: float32 [16, 2048], replicated, may hold values from -0.125 to 0.125
- teacher_mod: float32 [16, 3, 2048], replicated, may hold values from -3 to 3
- teacher_qkv: bfloat16 [2048, 3, 1024], P(None, None, 'mp'), may hold values from -1 to 1
- teacher_out: bfloat16 [2048, 1024], P(None, 'mp'), may hold values from -0.1875 to 0.1875
- student_embed: float32 [16, 2048], replicated, may hold values from -1.5 to 1.5
- student_final: float32 [16, 2048], replicated, may hold values from -0.125 to 0.125
- student_mod: float32 [8, 3, 2048], replicated, may hold values from -3 to 3
- student_qkv: bfloat16 [2048, 3, 1024], P('dp', None, 'mp'), may hold values from -1 to 1
- student_out: bfloat16 [2048, 1024], P('dp', 'mp'), may hold values from -0.1875 to 0.1875
- moment_qkv: float32 [2048, 3, 1024], P('dp', None, 'mp'), may hold values from -2 to 2
- second_qkv: float32 [2048, 3, 1024], P('dp', None, 'mp'), may hold values from 0.05 to 0.5
- moment_out: float32 [2048, 1024], P('dp', 'mp'), may hold values from -2 to 2
- second_out: float32 [2048, 1024], P('dp', 'mp'), may hold values from 0.05 to 0.5
Outputs:
- new_moment_qkv: float32 [2048, 3, 1024], P('dp', None, 'mp')
- new_second_qkv: float32 [2048, 3, 1024], P('dp', None, 'mp')
- update_qkv: float32 [2048, 3, 1024], P('dp', None, 'mp')
- new_moment_out: float32 [2048, 1024], P('dp', 'mp')
- new_second_out: float32 [2048, 1024], P('dp', 'mp')
- update_out: float32 [2048, 1024], P('dp', 'mp')
- loss: float32 [], replicated
All inputs are finite; a program needn't handle non-finite values.
Results may differ from a plain program's by a relative error of at most 0.00035.
Values may be sent and summed in bfloat16 or wider, within the bound.
A program may use at most 128 MiB of HBM per device.

v0:
```python
import math
import jax
import jax.numpy as jnp
from jax import lax
from jax.sharding import Mesh
from jax.sharding import PartitionSpec as P

D = 2048
HS = 64
INNER = 1024
PATCH_CH = 16
SEQ = 256
LATENT = 4096
K = 8
TGRID = 16
NBUCKET = 8
DP = ("dp_0", "dp_1", "dp_2", "dp_3")
DP_MP = ("dp_0", "dp_1", "dp_2", "dp_3", "mp")
LN_EPS = 0.01
BETA_ONE = 0.9
BETA_TWO = 0.99
ADAM_EPS = 1e-08


def in_blocks(shard, dim, devices):
    before, after = (shard.shape[:dim], shard.shape[dim + 1 :])
    return jnp.moveaxis(shard.reshape(*before, devices, -1, *after), dim, 0)


def summed_on_arrival(shard, axis, dim):
    devices = lax.axis_size(axis)
    parts = lax.all_to_all(in_blocks(shard, dim, devices), axis, 0, 0, tiled=True)
    return jnp.sum(parts, axis=0)


def side_by_side(arrays, axis, dim, along):
    widths = [math.prod(a.shape[along:]) for a in arrays]
    both = jnp.concatenate(
        [a.reshape(*a.shape[:along], w) for a, w in zip(arrays, widths)], axis=along
    )
    whole = lax.all_gather(both, axis, axis=dim, tiled=True)
    parts = jnp.split(whole, [sum(widths[:k]) for k in range(1, len(widths))], axis=along)
    return tuple((b.reshape(*whole.shape[:along], *a.shape[along:]) for a, b in zip(arrays, parts)))


def in_order(parts, dim):
    parts = jnp.moveaxis(parts, 0, dim)
    dims = parts.shape
    return parts.reshape(*dims[:dim], dims[dim] * dims[dim + 1], *dims[dim + 2 :])


def sent_to_all(shard, axis):
    copies = jnp.broadcast_to(shard, (lax.axis_size(axis), *shard.shape))
    return lax.all_to_all(copies, axis, split_axis=0, concat_axis=0, tiled=True)


def gathered_copies(shard, axis, dim):
    return in_order(sent_to_all(shard, axis), dim)


def by_axis(shard, axes):
    for axis in axes:
        shard = lax.psum(shard, axis)
    return shard


def summed_rows_2(shard, chips, core, dim):
    sizes = (lax.axis_size(chips), lax.axis_size(core))
    parts = in_blocks(shard, dim, sizes[0] * sizes[1])
    inside = parts.shape[1:]
    parts = parts.reshape(*sizes, *inside).swapaxes(0, 1).reshape(-1, *inside)
    parts = lax.psum_scatter(parts, core, scatter_dimension=0, tiled=True)
    return lax.psum_scatter(parts, chips, scatter_dimension=0, tiled=True)[0]


def plan():
    grid = jnp.arange(TGRID + 1, dtype=jnp.float32)
    lamb = 6.0 - 12.0 * grid / TGRID
    return (jnp.sqrt(jax.nn.sigmoid(lamb)), jnp.sqrt(jax.nn.sigmoid(-lamb)))


def positions():
    index = jnp.arange(SEQ, dtype=jnp.float32)[:, None]
    half = D // 2
    freqs = jnp.exp(-math.log(10000.0) * jnp.arange(half, dtype=jnp.float32) / half)
    angles = index * freqs[None, :]
    return jnp.concatenate([jnp.sin(angles), jnp.cos(angles)], axis=1)


def normalize(values):
    center = values - jnp.mean(values, axis=-1, keepdims=True)
    inverse = lax.rsqrt(jnp.mean(center * center, axis=-1, keepdims=True) + LN_EPS)
    return (center * inverse, inverse)


def norm_back(upstream, normed, inverse):
    first_mean = jnp.mean(upstream, axis=-1, keepdims=True)
    second_mean = jnp.mean(upstream * normed, axis=-1, keepdims=True)
    return (upstream - first_mean - normed * second_mean) * inverse


def one_hot_rows(index, width):
    return (index[:, None] == jnp.arange(width, dtype=jnp.int32)[None, :]).astype(jnp.float32)


def per_device(
    clean_latent,
    noise_draw,
    timestep,
    bucket,
    bucket_weights,
    teacher_embed,
    teacher_final,
    teacher_mod,
    teacher_qkv,
    teacher_out,
    student_embed,
    student_final,
    student_mod,
    student_qkv,
    student_out,
    moment_qkv,
    second_qkv,
    moment_out,
    second_out,
):
    samples = clean_latent.shape[0]
    rows_all = samples * SEQ
    local_inner = teacher_out.shape[1]
    local_heads = local_inner // HS
    count = rows_all // lax.axis_size("mp")
    start = lax.axis_index("mp") * count

    def take(values):
        return lax.dynamic_slice_in_dim(values, start, count, 0)

    alphas, sigmas = plan()
    table = jnp.stack([alphas, sigmas], axis=1)

    def coefficients(tau):
        picked = jnp.dot(one_hot_rows(tau, TGRID + 1), table, precision=lax.Precision.HIGHEST)
        picked = jnp.repeat(picked, SEQ, axis=0)
        return (picked[:, 0:1], picked[:, 1:2])

    def modulation(mod_table, index, length):
        picked = jnp.dot(
            one_hot_rows(index, length),
            mod_table.reshape(length, 3 * D),
            precision=lax.Precision.HIGHEST,
        )
        return picked.reshape(samples, 3, D)

    def gate_rows(modrows):
        return take(jnp.repeat(modrows[:, 2], SEQ, axis=0))

    placed = positions()

    def front(latent, modrows, embed, w_qkv, w_out):
        hidden = (
            jnp.dot(latent, embed, precision=lax.Precision.HIGHEST).reshape(samples, SEQ, D)
            + placed[None]
        )
        normed, unused = normalize(hidden)
        shaped = (
            (normed * (1.0 + modrows[:, None, 1]) + modrows[:, None, 0])
            .astype(jnp.bfloat16)
            .reshape(rows_all, D)
        )
        hidden = hidden.reshape(rows_all, D)
        packed = jnp.dot(
            shaped, w_qkv.reshape(D, 3 * local_inner), preferred_element_type=jnp.float32
        )
        packed = packed.astype(jnp.bfloat16).reshape(samples, SEQ, 3, local_heads, HS)
        queries = packed[:, :, 0]
        keys_all = packed[:, :, 1]
        values = packed[:, :, 2]
        scores = jnp.einsum(
            "sqhd,skhd->shqk", queries, keys_all, preferred_element_type=jnp.float32
        ) / math.sqrt(HS)
        highest = jnp.max(scores, axis=-1, keepdims=True)
        expos = jnp.exp(scores - highest)
        weights = expos / jnp.sum(expos, axis=-1, keepdims=True)
        rounded = weights.astype(jnp.bfloat16)
        attended = jnp.einsum(
            "shqk,skhd->sqhd", rounded, values, preferred_element_type=jnp.float32
        )
        attended = attended.astype(jnp.bfloat16).reshape(rows_all, local_inner)
        projected = lax.dot_general(
            attended, w_out, (((1,), (1,)), ((), ())), preferred_element_type=jnp.float32
        )
        return (hidden, shaped, queries, keys_all, values, weights, rounded, attended, projected)

    def reduce_heads(projected):
        return summed_on_arrival(projected, "mp", 0)

    def tail(hidden, modrows, projected, final):
        mixed = take(hidden) + gate_rows(modrows) * reduce_heads(projected)
        normed, inverse = normalize(mixed)
        predicted = lax.dot_general(
            normed, final, (((1,), (1,)), ((), ())), precision=lax.Precision.HIGHEST
        )
        return (predicted, normed, inverse)

    def teacher_eps(latent, modrows):
        parts = front(latent, modrows, teacher_embed, teacher_qkv, teacher_out)
        return tail(parts[0], modrows, parts[8], teacher_final)[0]

    whole_qkv, whole_out = side_by_side((student_qkv, student_out), DP, 0, 1)
    first = 2 * timestep
    middle = first - 1
    last = first - 2
    a_first, s_first = coefficients(first)
    a_middle, s_middle = coefficients(middle)
    a_last, s_last = coefficients(last)
    clean_rows = clean_latent.reshape(rows_all, PATCH_CH)
    noise_rows = noise_draw.reshape(rows_all, PATCH_CH)
    latent0 = a_first * clean_rows + s_first * noise_rows
    mine0 = take(latent0)
    af_mine, sf_mine = (take(a_first), take(s_first))
    am_mine, sm_mine = (take(a_middle), take(s_middle))
    al_mine, sl_mine = (take(a_last), take(s_last))
    eps_zero = teacher_eps(latent0, modulation(teacher_mod, first - 1, TGRID))
    next_mine = am_mine * (mine0 - sf_mine * eps_zero) / af_mine + sm_mine * eps_zero
    latent1 = gathered_copies(next_mine, "mp", 0)
    eps_one = teacher_eps(latent1, modulation(teacher_mod, middle - 1, TGRID))
    latent2 = al_mine * (take(latent1) - sm_mine * eps_one) / am_mine + sl_mine * eps_one
    target = (mine0 - af_mine / al_mine * latent2) / (sf_mine - af_mine * sl_mine / al_mine)
    student_rows_mod = modulation(student_mod, timestep - 1, K)
    hidden, shaped, queries, keys_all, values, weights, rounded, attended, projected = front(
        latent0, student_rows_mod, student_embed, whole_qkv, whole_out
    )
    predicted, normed, inverse = tail(hidden, student_rows_mod, projected, student_final)
    sample_weight = jnp.dot(
        one_hot_rows(bucket, NBUCKET), bucket_weights, precision=lax.Precision.HIGHEST
    )
    row_weight = take(jnp.repeat(sample_weight, SEQ, axis=0)[:, None])
    error = predicted - target
    loss_part = jnp.sum(row_weight * error * error)
    d_pred = 2.0 * row_weight * error
    d_normed = jnp.dot(d_pred, student_final, precision=lax.Precision.HIGHEST)
    d_mixed = norm_back(d_normed, normed, inverse)
    d_proj_mine = (gate_rows(student_rows_mod) * d_mixed).astype(jnp.bfloat16)
    d_proj = gathered_copies(d_proj_mine, "mp", 0)
    loss_sum = by_axis(loss_part, DP_MP)
    d_attn = jnp.dot(d_proj, whole_out, preferred_element_type=jnp.float32).astype(jnp.bfloat16)
    d_attn = d_attn.reshape(samples, SEQ, local_heads, HS)
    d_prob = jnp.einsum("sqhd,skhd->shqk", d_attn, values, preferred_element_type=jnp.float32)
    d_score = (
        weights * (d_prob - jnp.sum(weights * d_prob, axis=-1, keepdims=True)) / math.sqrt(HS)
    ).astype(jnp.bfloat16)
    d_query = jnp.einsum(
        "shqk,skhd->sqhd", d_score, keys_all, preferred_element_type=jnp.float32
    ).astype(jnp.bfloat16)
    d_key = jnp.einsum(
        "shqk,sqhd->skhd", d_score, queries, preferred_element_type=jnp.float32
    ).astype(jnp.bfloat16)
    d_value = jnp.einsum(
        "shqk,sqhd->skhd", rounded, d_attn, preferred_element_type=jnp.float32
    ).astype(jnp.bfloat16)
    d_pack = jnp.stack([d_query, d_key, d_value], axis=2).reshape(rows_all, 3 * local_inner)
    own_rows = D // lax.axis_size(DP)
    piece = shaped
    grad_qkv = lax.psum_scatter(
        lax.dot_general(
            piece, d_pack, (((0,), (0,)), ((), ())), preferred_element_type=jnp.float32
        ),
        DP,
        scatter_dimension=0,
        tiled=True,
    ).reshape(own_rows, 3, local_inner)
    piece = d_proj
    grad_out = summed_rows_2(
        lax.dot_general(
            piece, attended, (((0,), (0,)), ((), ())), preferred_element_type=jnp.float32
        ),
        ("dp_0", "dp_1", "dp_2"),
        "dp_3",
        0,
    )
    squares = jnp.sum(grad_qkv * grad_qkv) + jnp.sum(grad_out * grad_out)
    squares = by_axis(squares, DP_MP)
    rms_value = jnp.sqrt(squares / (4 * D * INNER))
    factor = 1.0 / jnp.maximum(rms_value, 1.0)

    def adam(moment, second, grad):
        normed_grad = grad * factor
        new_moment = BETA_ONE * moment + (1.0 - BETA_ONE) * normed_grad
        new_second = BETA_TWO * second + (1.0 - BETA_TWO) * normed_grad * normed_grad
        return (new_moment, new_second, new_moment / (jnp.sqrt(new_second) + ADAM_EPS))

    mq, vq, uq = adam(moment_qkv, second_qkv, grad_qkv)
    mo, vo, uo = adam(moment_out, second_out, grad_out)
    loss = loss_sum / (samples * lax.axis_size(DP) * LATENT)
    return (mq, vq, uq, mo, vo, uo, loss)


def solution(mesh):
    torus = Mesh(
        mesh.devices.reshape(4, 4, 2, 2, mesh.shape["mp"]), ("dp_0", "dp_1", "dp_2", "dp_3", "mp")
    )
    in_specs = (
        P(DP, None),
        P(DP, None),
        P(DP),
        P(DP),
        P(),
        P(),
        P(),
        P(),
        P(None, None, "mp"),
        P(None, "mp"),
        P(),
        P(),
        P(),
        P(DP, None, "mp"),
        P(DP, "mp"),
        P(DP, None, "mp"),
        P(DP, None, "mp"),
        P(DP, "mp"),
        P(DP, "mp"),
    )
    out_specs = (
        P(DP, None, "mp"),
        P(DP, None, "mp"),
        P(DP, None, "mp"),
        P(DP, "mp"),
        P(DP, "mp"),
        P(DP, "mp"),
        P(),
    )
    return jax.shard_map(
        per_device, mesh=torus, in_specs=in_specs, out_specs=out_specs, check_vma=False
    )
```

profile of v0, /device:TPU:10, one launch (start us, length us, event | category | flops | bytes accessed | tf_op | source)
XLA Modules:
  0.0 784.5 jit_solution(3109990404546934198)
XLA Ops:
  8.3 1.4 pad_maximum_fusion.2
  11.1 2.1 add_reduce_fusion
  13.3 8.9 %copy.110 = bf16[2048,3,512]{0,2,1:T(8,128)(2,1)} copy(bf16[2048,3,512]{2,0,1:T(8,128)(2,1)} %param.27) | data formatting | bytes 12582912 | tf_op args[8]
  22.2 3.7 fusion.66
  25.9 2.0 fusion.162
  29.9 2.8 convolution_convert_fusion.1
  32.7 2.3 copy.111
  35.0 1.9 fusion.163
  36.8 2.9 fusion.45
  40.8 2.1 fusion.11
  42.9 5.8 all-to-all-start.1
  48.9 3.2 fusion.160
  52.1 1.3 copy-done.2
  57.0 18.7 %all-to-all-done.1 = f32[2,128,2048]{2,1,0:T(8,128)} async-done(((f32[2,128,2048]{2,1,0:T(8,128)}), f32[2,128,2048]{2,1,0:T(8,128)}, u32[]{:S(2)}, u32[]{:S(2)}) %all-to-all-start.1) | async-done | bytes 2097184 | tf_op jit(solution)/shard_map/all_to_all | solution.py:32
  75.7 2.8 reduce_sum.225
  78.6 1.8 fusion.152
  80.7 3.6 multiply_add_fusion.3
  84.9 3.2 all-to-all-start.2
  93.5 3.3 fusion.164
  98.1 4.8 convolution_convert_fusion
  102.8 1.2 copy.115
  104.1 1.9 fusion.165
  107.2 2.1 fusion.9
  109.2 5.1 all-to-all-start.3
  115.6 24.7 %all-to-all-done.3 = f32[2,128,2048]{2,1,0:T(8,128)} async-done(((f32[2,128,2048]{2,1,0:T(8,128)}), f32[2,128,2048]{2,1,0:T(8,128)}, u32[]{:S(2)}, u32[]{:S(2)}) %all-to-all-start.3) | async-done | bytes 2097184 | tf_op jit(solution)/shard_map/all_to_all | solution.py:32
  140.3 2.8 reduce_sum.231
  143.1 5.6 fusion.6
  148.7 1.4 copy.105
  150.1 2.2 fusion.161
  152.3 1.9 convolution_convert_fusion.5
  154.3 3.7 fusion.13
  158.0 4.8 all-to-all-start
  162.9 1.8 fusion.151
  164.9 1.6 fusion.48
  166.6 21.4 %all-to-all-done = f32[2,128,2048]{2,1,0:T(8,128)} async-done(((f32[2,128,2048]{2,1,0:T(8,128)}), f32[2,128,2048]{2,1,0:T(8,128)}, u32[]{:S(2)}, u32[]{:S(2)}) %all-to-all-start) | async-done | bytes 2097184 | tf_op jit(solution)/shard_map/all_to_all | solution.py:32
  188.0 2.9 reduce_sum.219
  190.9 1.5 fusion.153
  192.7 4.7 fusion.104
  197.4 1.3 fusion.146
  198.7 1.5 multiply_convert_fusion.1
  200.2 2.1 copy.118
  202.3 1.2 broadcast_in_dim.5
  203.5 16.2 %all_to_all.25 = bf16[2,128,2048]{1,2,0:T(8,128)(2,1)} all-to-all(bf16[2,128,2048]{1,2,0:T(8,128)(2,1)S(1)} %broadcast_in_dim.5), channel_id=1, replica_groups=mesh['dp_0'=4,'dp_1'=4,'dp_2'=2,'dp_3'=2,'mp'=2] {'mp'}, dimensions={0} | all-to-all | bytes 2097152 | tf_op jit(solution)/shard_map/all_to_all | solution.py:54
  219.7 1.5 copy.119
  221.2 1.4 copy.124
  222.6 2.0 convolution_bitcast_fusion
  224.5 2.5 copy.126
  227.1 29.4 %reduce-scatter.6.cloned.1.call-done = f32[32,32,512]{2,1,0:T(8,128)} async-done(((f32[64,32,512]{2,1,0:T(8,128)}), f32[32,32,512]{2,1,0:T(8,128)}) %reduce-scatter.6.cloned.1.call-update) | async-done | bytes 2097168 | tf_op jit(solution)/shard_map/reduce_scatter | solution.py:72
  256.8 2.3 fusion.36
  259.2 2.9 fusion.91
  262.1 4.5 fusion.42
  266.6 5.2 fusion.39
  271.8 2.1 fusion.47
  274.0 6.6 fusion.145
  280.6 126.1 %reduce-scatter.8.cloned.1.call-done = f32[1,32,512]{2,1,0:T(8,128)} async-done(((f32[32,32,512]{2,1,0:T(8,128)}), f32[1,32,512]{2,1,0:T(8,128)}) %reduce-scatter.8.cloned.1.call-update) | async-done | bytes 65552 | tf_op jit(solution)/shard_map/reduce_scatter | solution.py:73
  406.8 1.5 multiply_reduce_fusion.12
  408.3 276.5 %reduce-scatter.4.cloned.1.call-done = f32[32,1536]{1,0:T(8,128)} async-done(((f32[2048,1536]{1,0:T(8,128)}), f32[32,1536]{1,0:T(8,128)}) %reduce-scatter.4.cloned.1.call-update) | async-done | bytes 196624 | tf_op jit(solution)/shard_map/reduce_scatter | solution.py:263
  684.8 1.7 multiply_reduce_fusion.11
  687.9 47.4 %all-reduce.1 = (f32[]{:T(128)}, f32[]{:T(128)}) all-reduce(f32[]{:T(128)S(6)} %add.251, f32[]{:T(128)} %get-tuple-element.75), channel_id=1, replica_groups=mesh['dp_0'=4,'dp_1'=4,'dp_2'=2,'dp_3'=2,'mp'=2] {'dp_0'}, use_global_device_ids=true, to_apply=%region_29.0 | all-reduce | flops 2 | bytes 16 | tf_op jit(solution)/shard_map/psum | solution.py:63
  735.2 18.8 %all-reduce = (f32[]{:T(128)}, f32[]{:T(128)}) all-reduce(f32[]{:T(128)} %get-tuple-element.32, f32[]{:T(128)} %get-tuple-element.33), channel_id=1, replica_groups=mesh['dp_0'=4,'dp_1'=4,'dp_2'=2,'dp_3'=2,'mp'=2] {'dp_1'}, use_global_device_ids=true, to_apply=%region_30.0 | all-reduce | flops 2 | bytes 16 | tf_op jit(solution)/shard_map/psum | solution.py:63
  754.1 5.5 all-reduce.4
  759.6 3.1 all-reduce.3
  762.7 7.0 all-reduce.2
  771.6 1.4 add_divide_fusion
  (137 shorter events, 18.7 us)
Async XLA Ops:
  7.2 33.6 %copy-start = (bf16[2048,512]{1,0:T(8,128)(2,1)S(1)}, bf16[2048,512]{1,0:T(8,128)(2,1)}, u32[]{:S(2)}) copy-start(bf16[2048,512]{1,0:T(8,128)(2,1)} %param.28) | copy-start | bytes 6291460
  7.2 135.9 %all-gather.2.cloned.1.call-start = ((), (), s32[]{:S(2)}) async-start(), calls=%async_computation.8 | async-start | bytes 8519680 | tf_op jit(solution)/shard_map/all_gather | solution.py:41
  22.2 3.7 copy-start.13
  25.9 2.0 copy-start.4
  25.9 2.4 copy-start.8
  25.9 4.0 copy-start.7
  27.9 1.4 copy-start.5
  42.9 6.0 copy-start.21
  42.9 32.9 %all-to-all-start.1 = ((f32[2,128,2048]{2,1,0:T(8,128)}), f32[2,128,2048]{2,1,0:T(8,128)}, u32[]{:S(2)}, u32[]{:S(2)}) async-start(f32[2,128,2048]{2,1,0:T(8,128)} %fusion.11), calls=%async_computation.1 | async-start | bytes 4194304 | tf_op jit(solution)/shard_map/all_to_all | solution.py:32
  52.1 1.3 copy-start.2
  52.1 1.7 copy-start.19
  52.1 1.9 copy-start.9
  52.1 91.0 %copy-start.29 = (f32[256]{0:T(256)}, f32[256]{0:T(256)S(1)}, u32[]{:S(2)}) copy-start(f32[256]{0:T(256)S(1)} %broadcast_multiply_fusion.3) | copy-start | bytes 3076
  53.8 89.3 %copy-start.31 = (f32[256]{0:T(256)}, f32[256]{0:T(256)S(1)}, u32[]{:S(2)}) copy-start(f32[256]{0:T(256)S(1)} %add_rsqrt_fusion.2) | copy-start | bytes 3076
  55.0 25.7 %copy-start.22 = (f32[128,16]{0,1:T(8,128)}, f32[128,16]{0,1:T(8,128)S(1)}, u32[]{:S(2)}) copy-start(f32[128,16]{0,1:T(8,128)S(1)} %copy.148) | copy-start | bytes 24580
  78.6 2.1 copy-start.16
  78.6 9.6 %copy-start.33 = (f32[8]{0:T(128)S(1)}, f32[8]{0:T(128)}, u32[]{:S(2)}) copy-start(f32[8]{0:T(128)} %param.23) | copy-start | bytes 100
  78.6 14.9 %copy-start.14 = (f32[16,2048]{1,0:T(8,128)S(1)}, f32[16,2048]{1,0:T(8,128)}, u32[]{:S(2)}) copy-start(f32[16,2048]{1,0:T(8,128)} %param.24) | copy-start | bytes 393220
  84.9 8.6 %all-to-all-start.2 = ((f32[2,128,16]{1,2,0:T(8,128)}), f32[2,128,16]{1,2,0:T(8,128)S(1)}, u32[]{:S(2)}, u32[]{:S(2)}) async-start(f32[2,128,16]{1,2,0:T(8,128)} %broadcast_in_dim.4), calls=%async_computation.2 | async-start | bytes 32768 | tf_op jit(solution)/shard_map/all_to_all | solution.py:54
  96.7 1.4 copy-start.6
  104.1 1.9 copy-start.12
  109.2 31.0 %all-to-all-start.3 = ((f32[2,128,2048]{2,1,0:T(8,128)}), f32[2,128,2048]{2,1,0:T(8,128)}, u32[]{:S(2)}, u32[]{:S(2)}) async-start(f32[2,128,2048]{2,1,0:T(8,128)} %fusion.9), calls=%async_computation.3 | async-start | bytes 4194304 | tf_op jit(solution)/shard_map/all_to_all | solution.py:32
  114.3 28.8 %copy-start.3 = (f32[256,2048]{1,0:T(8,128)S(1)}, f32[256,2048]{1,0:T(8,128)}, u32[]{:S(2)}) copy-start(f32[256,2048]{1,0:T(8,128)} %copy-done.2) | copy-start | bytes 6291460
  150.1 4.1 copy-start.10
  152.3 1.9 copy-start.34
  158.0 29.9 %all-to-all-start = ((f32[2,128,2048]{2,1,0:T(8,128)}), f32[2,128,2048]{2,1,0:T(8,128)}, u32[]{:S(2)}, u32[]{:S(2)}) async-start(f32[2,128,2048]{2,1,0:T(8,128)} %fusion.13), calls=%async_computation | async-start | bytes 4194304 | tf_op jit(solution)/shard_map/all_to_all | solution.py:32
  162.9 93.6 %reduce-scatter.6.cloned.1.call-start = ((), (), s32[]{:S(2)}) async-start(), calls=%async_computation.10 | async-start | bytes 6291456 | tf_op jit(solution)/shard_map/reduce_scatter | solution.py:72
  166.6 24.3 %copy-start.24 = (f32[1,1,2048]{2,0,1:T(1,128)S(1)}, f32[1,1,2048]{2,0,1:T(1,128)}, u32[]{:S(2)}) copy-start(f32[1,1,2048]{2,0,1:T(1,128)} %get-tuple-element.56) | copy-start | bytes 24580
  190.9 1.8 copy-start.15
  190.9 1.8 copy-start.23
  190.9 1.8 copy-start.27
  190.9 1.8 copy-start.28
  227.0 179.7 %reduce-scatter.8.cloned.1.call-start = ((), (), s32[]{:S(2)}) async-start(), calls=%async_computation.11 | async-start | bytes 2162688 | tf_op jit(solution)/shard_map/reduce_scatter | solution.py:73
  256.5 428.3 %reduce-scatter.4.cloned.1.call-start = ((), (), s32[]{:S(2)}) async-start(), calls=%async_computation.9 | async-start | bytes 12779520 | tf_op jit(solution)/shard_map/reduce_scatter | solution.py:263
  259.1 3.0 copy-start.11
  259.1 3.0 copy-start.35
  271.8 2.1 copy-start.18
  271.8 2.2 copy-start.30
  271.8 2.2 copy-start.32
  280.6 491.0 %copy-start.20 = (f32[32,3,512]{2,0,1:T(8,128)S(1)}, f32[32,3,512]{2,0,1:T(8,128)}, u32[]{:S(2)}) copy-start(f32[32,3,512]{2,0,1:T(8,128)} %param.35) | copy-start | bytes 589828
  280.6 495.3 %copy-start.25 = (f32[32,512]{1,0:T(8,128)S(1)}, f32[32,512]{1,0:T(8,128)}, u32[]{:S(2)}) copy-start(f32[32,512]{1,0:T(8,128)} %param.37) | copy-start | bytes 196612
  280.6 495.3 %copy-start.26 = (f32[32,512]{1,0:T(8,128)S(1)}, f32[32,512]{1,0:T(8,128)}, u32[]{:S(2)}) copy-start(f32[32,512]{1,0:T(8,128)} %param.36) | copy-start | bytes 196612
  406.8 369.1 %copy-start.17 = (f32[1,32,512]{2,1,0:T(8,128)S(1)}, f32[1,32,512]{2,1,0:T(8,128)}, u32[]{:S(2)}) copy-start(f32[1,32,512]{2,1,0:T(8,128)} %reduce-scatter.8.cloned.1.call-done) | copy-start | bytes 196612
  684.8 91.8 %copy-start.1 = (bf16[2048,512]{1,0:T(8,128)(2,1)S(1)}, bf16[2048,512]{1,0:T(8,128)(2,1)}, u32[]{:S(2)}) copy-start(bf16[2048,512]{1,0:T(8,128)(2,1)} %param.28) | copy-start | bytes 6291460
Sparse Core Ops, SparseCore 0:
  10.3 113.7 all-gather.1
  227.1 29.3 reduce-scatter.5
  258.9 147.8 reduce-scatter.7
  409.0 275.7 reduce-scatter.3
where the time goes:
time: 794 us; the launch traced here: 784 us
  waiting for transfers between devices  497 us (63%)
  blocking collectives  98.1 us (12%)
  matrix products  79.1 us (10%)
  local copies, waits for them, and re-layouts  35.3 us (4%)
  other arithmetic  31.2 us (4%)
  between operations  24.3 us (3%)
  starting transfers between devices  19.3 us (2%)
    reduce_scatter x1, waiting for transfers between devices, per_device(): lax.psum_scatter(lax.dot_general(piece, d_pack, (((0,), (0,)), ((), ())),...  277 us
    reduce_scatter x1, waiting for transfers between devices, summed_rows_2(): return lax.psum_scatter(parts, chips, scatter_dimension=0, tiled=True)[0]  126 us
    psum x5, blocking collectives, by_axis(): shard = lax.psum(shard, axis)  81.9 us
    all_to_all x3, waiting for transfers between devices, summed_on_arrival(): lax.all_to_all(in_blocks(shard, dim, devices), axis, 0, 0, tiled=True)  64.8 us
    reduce_scatter x1, waiting for transfers between devices, summed_rows_2(): parts = lax.psum_scatter(parts, core, scatter_dimension=0, tiled=True)  29.4 us
    all_to_all x1, blocking collectives, sent_to_all(): return lax.all_to_all(copies, axis, split_axis=0, concat_axis=0, tiled=True)  16.2 us
  transfers between devices with their start and end apart: 8, of which 7 were waited for; matrix products, arithmetic and copies ran while one was open for 12% of the time, Pallas kernels for 0%

commit v1 on v0

--- a/solution.py
+++ b/solution.py
@@ -22,6 +22,10 @@
 ADAM_EPS = 1e-08
 
 
+def group_pairs_all(s0, along_axis):
+    return jnp.sum(lax.all_gather(s0, axis_name=along_axis), axis=0)
+
+
 def in_blocks(shard, dim, devices):
     before, after = (shard.shape[:dim], shard.shape[dim + 1 :])
     return jnp.moveaxis(shard.reshape(*before, devices, -1, *after), dim, 0)
@@ -60,7 +64,7 @@
 
 def by_axis(shard, axes):
     for axis in axes:
-        shard = lax.psum(shard, axis)
+        shard = group_pairs_all(shard, axis)
     return shard
 
 

time: 794 us -> 810 us (1.020)
  local copies, waits for them, and re-layouts: 35.3 us -> 51.6 us
    psum x5 -> x0, blocking collectives: 81.9 us -> none  [by_axis(): shard = lax.psum(shard, axis)]
    unnamed x0 -> x5, blocking collectives: none -> 79.8 us
    unnamed x77 -> x114, local copies, waits for them, and re-layouts: 14.8 us -> 32.1 us
where the time goes in v1:
time: 810 us; the launch traced here: 800 us
  waiting for transfers between devices  497 us (61%)
  blocking collectives  96.1 us (12%)
  matrix products  80.3 us (10%)
  local copies, waits for them, and re-layouts  51.6 us (6%)
  other arithmetic  31.5 us (4%)
  between operations  24.5 us (3%)
  starting transfers between devices  19.5 us (2%)
    reduce_scatter x1, waiting for transfers between devices, per_device(): lax.psum_scatter(lax.dot_general(piece, d_pack, (((0,), (0,)), ((), ())),...  278 us
    reduce_scatter x1, waiting for transfers between devices, summed_rows_2(): return lax.psum_scatter(parts, chips, scatter_dimension=0, tiled=True)[0]  123 us
    unnamed x5, blocking collectives  79.8 us
    all_to_all x3, waiting for transfers between devices, summed_on_arrival(): lax.all_to_all(in_blocks(shard, dim, devices), axis, 0, 0, tiled=True)  65.9 us
    unnamed x114, local copies, waits for them, and re-layouts  32.1 us
    reduce_scatter x1, waiting for transfers between devices, summed_rows_2(): parts = lax.psum_scatter(parts, core, scatter_dimension=0, tiled=True)  30 us
    all_to_all x1, blocking collectives, sent_to_all(): return lax.all_to_all(copies, axis, split_axis=0, concat_axis=0, tiled=True)  16.3 us
  transfers between devices with their start and end apart: 8, of which 7 were waited for; matrix products, arithmetic and copies ran while one was open for 12% of the time, Pallas kernels for 0%

profile of v1, /device:TPU:10, one launch (start us, length us, event | category | flops | bytes accessed | tf_op | source)
XLA Modules:
  0.0 800.4 jit_solution(6539303337243164906)
XLA Ops:
  8.3 1.4 pad_maximum_fusion.2
  11.2 2.1 add_reduce_fusion
  13.4 8.9 %copy.110 = bf16[2048,3,512]{0,2,1:T(8,128)(2,1)} copy(bf16[2048,3,512]{2,0,1:T(8,128)(2,1)} %param.27) | data formatting | bytes 12582912 | tf_op args[8]
  22.2 3.7 fusion.66
  26.0 2.0 fusion.162
  29.9 2.8 convolution_convert_fusion.1
  32.7 2.3 copy.111
  35.0 1.9 fusion.163
  36.9 2.9 fusion.45
  40.8 2.1 fusion.11
  42.9 5.8 all-to-all-start.1
  48.9 3.2 fusion.160
  57.1 18.7 %all-to-all-done.1 = f32[2,128,2048]{2,1,0:T(8,128)} async-done(((f32[2,128,2048]{2,1,0:T(8,128)}), f32[2,128,2048]{2,1,0:T(8,128)}, u32[]{:S(2)}, u32[]{:S(2)}) %all-to-all-start.1) | async-done | bytes 2097184 | tf_op jit(solution)/shard_map/all_to_all | solution.py:36
  75.8 2.8 reduce_sum.315
  78.6 1.8 fusion.152
  80.7 3.6 multiply_add_fusion.3
  84.9 3.2 all-to-all-start.2
  93.5 3.3 fusion.164
  98.1 4.8 convolution_convert_fusion
  104.1 1.9 fusion.165
  107.2 2.1 fusion.9
  109.2 5.1 all-to-all-start.3
  115.6 24.8 %all-to-all-done.3 = f32[2,128,2048]{2,1,0:T(8,128)} async-done(((f32[2,128,2048]{2,1,0:T(8,128)}), f32[2,128,2048]{2,1,0:T(8,128)}, u32[]{:S(2)}, u32[]{:S(2)}) %all-to-all-start.3) | async-done | bytes 2097184 | tf_op jit(solution)/shard_map/all_to_all | solution.py:36
  140.4 1.8 reduce_sum.321
  142.3 5.6 fusion.6
  147.8 2.3 copy.105
  150.1 3.2 fusion.161
  153.4 2.7 convolution_convert_fusion.5
  157.1 3.8 fusion.13
  160.9 4.9 all-to-all-start
  165.9 1.4 fusion.151
  168.6 22.4 %all-to-all-done = f32[2,128,2048]{2,1,0:T(8,128)} async-done(((f32[2,128,2048]{2,1,0:T(8,128)}), f32[2,128,2048]{2,1,0:T(8,128)}, u32[]{:S(2)}, u32[]{:S(2)}) %all-to-all-start) | async-done | bytes 2097184 | tf_op jit(solution)/shard_map/all_to_all | solution.py:36
  191.0 1.8 reduce_sum.309
  193.7 4.8 fusion.104
  200.7 16.3 %all_to_all.25 = bf16[2,128,2048]{1,2,0:T(8,128)(2,1)} all-to-all(bf16[2,128,2048]{1,2,0:T(8,128)(2,1)S(1)} %broadcast_in_dim.5), channel_id=1, replica_groups=mesh['dp_0'=4,'dp_1'=4,'dp_2'=2,'dp_3'=2,'mp'=2] {'mp'}, dimensions={0} | all-to-all | bytes 2097152 | tf_op jit(solution)/shard_map/all_to_all | solution.py:58
  217.0 1.5 copy.119
  218.5 1.4 copy.124
  219.9 2.0 convolution_bitcast_fusion
  221.9 2.5 copy.126
  224.4 30.0 %reduce-scatter.6.cloned.1.call-done = f32[32,32,512]{2,1,0:T(8,128)} async-done(((f32[64,32,512]{2,1,0:T(8,128)}), f32[32,32,512]{2,1,0:T(8,128)}) %reduce-scatter.6.cloned.1.call-update) | async-done | bytes 2097168 | tf_op jit(solution)/shard_map/reduce_scatter | solution.py:76
  254.7 2.3 fusion.36
  257.2 2.9 fusion.91
  260.0 4.5 fusion.42
  264.5 5.2 fusion.39
  269.7 2.1 fusion.47
  271.9 6.6 fusion.145
  279.7 1.4 dynamic-update-slice.5
  281.1 123.3 %reduce-scatter.8.cloned.1.call-done = f32[1,32,512]{2,1,0:T(8,128)} async-done(((f32[32,32,512]{2,1,0:T(8,128)}), f32[1,32,512]{2,1,0:T(8,128)}) %reduce-scatter.8.cloned.1.call-update) | async-done | bytes 65552 | tf_op jit(solution)/shard_map/reduce_scatter | solution.py:77
  404.4 1.5 multiply_reduce_fusion.12
  406.0 277.5 %reduce-scatter.4.cloned.1.call-done = f32[32,1536]{1,0:T(8,128)} async-done(((f32[2048,1536]{1,0:T(8,128)}), f32[32,1536]{1,0:T(8,128)}) %reduce-scatter.4.cloned.1.call-update) | async-done | bytes 196624 | tf_op jit(solution)/shard_map/reduce_scatter | solution.py:267
  683.5 1.6 multiply_reduce_fusion.11
  687.7 47.7 %all-reduce.11 = (f32[4]{0:T(128)S(1)}, f32[4]{0:T(128)S(1)}) all-reduce(f32[4]{0:T(128)S(1)} %dynamic-update-slice, f32[4]{0:T(128)S(1)} %dynamic-update-slice.5), channel_id=1, replica_groups=mesh['dp_0'=4,'dp_1'=4,'dp_2'=2,'dp_3'=2,'mp'=2] {'dp_0'}, use_global_device_ids=true, to_apply=%add | all-reduce | flops 8 | bytes 64
  736.7 1.4 dynamic-update-slice.6
  738.1 1.4 dynamic-update-slice.1
  740.0 18.3 %all-reduce.10 = (f32[4]{0:T(128)S(1)}, f32[4]{0:T(128)S(1)}) all-reduce(f32[4]{0:T(128)S(1)} %dynamic-update-slice.1, f32[4]{0:T(128)S(1)} %dynamic-update-slice.6), channel_id=1, replica_groups=mesh['dp_0'=4,'dp_1'=4,'dp_2'=2,'dp_3'=2,'mp'=2] {'dp_1'}, use_global_device_ids=true, to_apply=%add.1 | all-reduce | flops 8 | bytes 64
  759.6 1.4 dynamic-update-slice.7
  761.0 1.4 dynamic-update-slice.2
  763.0 4.9 all-reduce.14
  769.1 1.4 dynamic-update-slice.8
  770.5 1.4 dynamic-update-slice.3
  772.5 2.4 all-reduce.13
  776.1 1.4 dynamic-update-slice.9
  777.5 1.4 dynamic-update-slice.4
  778.9 6.4 all-reduce.12
  (184 shorter events, 36.6 us)
Async XLA Ops:
  7.2 33.6 %copy-start = (bf16[2048,512]{1,0:T(8,128)(2,1)S(1)}, bf16[2048,512]{1,0:T(8,128)(2,1)}, u32[]{:S(2)}) copy-start(bf16[2048,512]{1,0:T(8,128)(2,1)} %param.28) | copy-start | bytes 6291460
  7.2 135.0 %all-gather.2.cloned.1.call-start = ((), (), s32[]{:S(2)}) async-start(), calls=%async_computation.8 | async-start | bytes 8519680 | tf_op jit(solution)/shard_map/all_gather | solution.py:45
  22.2 3.7 copy-start.13
  25.9 2.0 copy-start.4
  25.9 2.4 copy-start.8
  25.9 4.0 copy-start.7
  27.9 1.4 copy-start.5
  42.9 6.0 copy-start.22
  42.9 32.9 %all-to-all-start.1 = ((f32[2,128,2048]{2,1,0:T(8,128)}), f32[2,128,2048]{2,1,0:T(8,128)}, u32[]{:S(2)}, u32[]{:S(2)}) async-start(f32[2,128,2048]{2,1,0:T(8,128)} %fusion.11), calls=%async_computation.1 | async-start | bytes 4194304 | tf_op jit(solution)/shard_map/all_to_all | solution.py:36
  52.1 1.3 copy-start.2
  52.1 1.7 copy-start.19
  52.1 1.9 copy-start.9
  52.1 90.1 %copy-start.30 = (f32[256]{0:T(256)}, f32[256]{0:T(256)S(1)}, u32[]{:S(2)}) copy-start(f32[256]{0:T(256)S(1)} %broadcast_multiply_fusion.3) | copy-start | bytes 3076
  53.8 88.4 %copy-start.32 = (f32[256]{0:T(256)}, f32[256]{0:T(256)S(1)}, u32[]{:S(2)}) copy-start(f32[256]{0:T(256)S(1)} %add_rsqrt_fusion.2) | copy-start | bytes 3076
  55.0 25.7 %copy-start.23 = (f32[128,16]{0,1:T(8,128)}, f32[128,16]{0,1:T(8,128)S(1)}, u32[]{:S(2)}) copy-start(f32[128,16]{0,1:T(8,128)S(1)} %copy.148) | copy-start | bytes 24580
  78.6 2.1 copy-start.16
  78.6 9.5 %copy-start.34 = (f32[8]{0:T(128)S(1)}, f32[8]{0:T(128)}, u32[]{:S(2)}) copy-start(f32[8]{0:T(128)} %param.23) | copy-start | bytes 100
  78.6 14.9 %copy-start.14 = (f32[16,2048]{1,0:T(8,128)S(1)}, f32[16,2048]{1,0:T(8,128)}, u32[]{:S(2)}) copy-start(f32[16,2048]{1,0:T(8,128)} %param.24) | copy-start | bytes 393220
  84.9 8.6 %all-to-all-start.2 = ((f32[2,128,16]{1,2,0:T(8,128)}), f32[2,128,16]{1,2,0:T(8,128)S(1)}, u32[]{:S(2)}, u32[]{:S(2)}) async-start(f32[2,128,16]{1,2,0:T(8,128)} %broadcast_in_dim.4), calls=%async_computation.2 | async-start | bytes 32768 | tf_op jit(solution)/shard_map/all_to_all | solution.py:58
  96.7 1.4 copy-start.6
  104.1 1.9 copy-start.12
  109.2 31.1 %all-to-all-start.3 = ((f32[2,128,2048]{2,1,0:T(8,128)}), f32[2,128,2048]{2,1,0:T(8,128)}, u32[]{:S(2)}, u32[]{:S(2)}) async-start(f32[2,128,2048]{2,1,0:T(8,128)} %fusion.9), calls=%async_computation.3 | async-start | bytes 4194304 | tf_op jit(solution)/shard_map/all_to_all | solution.py:36
  114.3 27.9 %copy-start.3 = (f32[256,2048]{1,0:T(8,128)S(1)}, f32[256,2048]{1,0:T(8,128)}, u32[]{:S(2)}) copy-start(f32[256,2048]{1,0:T(8,128)} %copy-done.2) | copy-start | bytes 6291460
  153.4 2.7 copy-start.40
  160.9 5.0 copy-start.29
  160.9 30.1 %all-to-all-start = ((f32[2,128,2048]{2,1,0:T(8,128)}), f32[2,128,2048]{2,1,0:T(8,128)}, u32[]{:S(2)}, u32[]{:S(2)}) async-start(f32[2,128,2048]{2,1,0:T(8,128)} %fusion.13), calls=%async_computation | async-start | bytes 4194304 | tf_op jit(solution)/shard_map/all_to_all | solution.py:36
  165.8 88.6 %reduce-scatter.6.cloned.1.call-start = ((), (), s32[]{:S(2)}) async-start(), calls=%async_computation.10 | async-start | bytes 6291456 | tf_op jit(solution)/shard_map/reduce_scatter | solution.py:76
  167.6 25.2 %copy-start.25 = (f32[1,1,2048]{2,0,1:T(1,128)S(1)}, f32[1,1,2048]{2,0,1:T(1,128)}, u32[]{:S(2)}) copy-start(f32[1,1,2048]{2,0,1:T(1,128)} %get-tuple-element.56) | copy-start | bytes 24580
  192.8 0.9 copy-start.15
  192.8 0.9 copy-start.24
  192.9 0.9 copy-start.28
  217.0 2.9 copy-start.11
  224.4 180.1 %reduce-scatter.8.cloned.1.call-start = ((), (), s32[]{:S(2)}) async-start(), calls=%async_computation.11 | async-start | bytes 2162688 | tf_op jit(solution)/shard_map/reduce_scatter | solution.py:77
  254.4 429.1 %reduce-scatter.4.cloned.1.call-start = ((), (), s32[]{:S(2)}) async-start(), calls=%async_computation.9 | async-start | bytes 12779520 | tf_op jit(solution)/shard_map/reduce_scatter | solution.py:267
  257.0 3.0 copy-start.10
  257.0 3.0 copy-start.41
  269.7 2.1 copy-start.18
  269.7 2.2 copy-start.31
  269.7 2.2 copy-start.33
  278.5 0.7 copy-start.39
  278.5 408.7 %copy-start.38 = (u32[128]{0:T(128)S(1)}, u32[128]{0:T(128)}, u32[]{:S(2)}) copy-start(u32[128]{0:T(128)} %constant.109) | copy-start | bytes 1540
  278.5 461.0 %copy-start.37 = (u32[128]{0:T(128)S(1)}, u32[128]{0:T(128)}, u32[]{:S(2)}) copy-start(u32[128]{0:T(128)} %constant.114) | copy-start | bytes 1540
  278.5 483.9 %copy-start.36 = (u32[128]{0:T(128)S(1)}, u32[128]{0:T(128)}, u32[]{:S(2)}) copy-start(u32[128]{0:T(128)} %constant.119) | copy-start | bytes 1540
  278.5 493.4 %copy-start.35 = (u32[128]{0:T(128)S(1)}, u32[128]{0:T(128)}, u32[]{:S(2)}) copy-start(u32[128]{0:T(128)} %constant.124) | copy-start | bytes 1540
  278.5 509.3 %copy-start.20 = (f32[32,3,512]{2,0,1:T(8,128)S(1)}, f32[32,3,512]{2,0,1:T(8,128)}, u32[]{:S(2)}) copy-start(f32[32,3,512]{2,0,1:T(8,128)} %param.35) | copy-start | bytes 589828
  278.5 509.3 %copy-start.21 = (f32[32,3,512]{2,0,1:T(8,128)S(1)}, f32[32,3,512]{2,0,1:T(8,128)}, u32[]{:S(2)}) copy-start(f32[32,3,512]{2,0,1:T(8,128)} %param.34) | copy-start | bytes 589828
  278.6 513.2 %copy-start.26 = (f32[32,512]{1,0:T(8,128)S(1)}, f32[32,512]{1,0:T(8,128)}, u32[]{:S(2)}) copy-start(f32[32,512]{1,0:T(8,128)} %param.37) | copy-start | bytes 196612
  278.6 513.2 %copy-start.27 = (f32[32,512]{1,0:T(8,128)S(1)}, f32[32,512]{1,0:T(8,128)}, u32[]{:S(2)}) copy-start(f32[32,512]{1,0:T(8,128)} %param.36) | copy-start | bytes 196612
  404.4 387.4 %copy-start.17 = (f32[1,32,512]{2,1,0:T(8,128)S(1)}, f32[1,32,512]{2,1,0:T(8,128)}, u32[]{:S(2)}) copy-start(f32[1,32,512]{2,1,0:T(8,128)} %reduce-scatter.8.cloned.1.call-done) | copy-start | bytes 196612
  687.7 104.7 %copy-start.1 = (bf16[2048,512]{1,0:T(8,128)(2,1)S(1)}, bf16[2048,512]{1,0:T(8,128)(2,1)}, u32[]{:S(2)}) copy-start(bf16[2048,512]{1,0:T(8,128)(2,1)} %param.28) | copy-start | bytes 6291460
Sparse Core Ops, SparseCore 0:
  10.3 113.5 all-gather.1
  224.5 29.8 reduce-scatter.5
  256.8 147.5 reduce-scatter.7
  406.7 276.7 reduce-scatter.3
